TPU v7x, 32 devices: a whole 2x2x4 slice. The times are simulated.
32 devices in a mesh: section: 4 (over y, x), seq: 2 (over core), exp: 4 (over z).
Axes of the slice: x: 2, y: 2, z: 4, core: 2. Of those that a mesh axis runs over, the one named last changes fastest.
Arguments:
- latent: bfloat16 [8, 8, 64, 384], P('section', 'seq', 'exp'), may hold values from -6 to 6
- cotangent: bfloat16 [8, 8, 64, 384], P('section', 'seq', 'exp'), may hold values from -6 to 6
- gain_one: float32 [384], replicated, may hold values from 0.5 to 2
- gain_two: float32 [384], replicated, may hold values from 0.5 to 2
- kernel_one: bfloat16 [3, 3, 3, 384, 384], P(None, None, None, 'exp'), may hold values from -0.0625 to 0.0625
- kernel_two: bfloat16 [3, 3, 3, 384, 384], P(None, None, None, 'exp'), may hold values from -0.0625 to 0.0625
Outputs:
- block_out: bfloat16 [8, 8, 64, 384], P('section', 'seq', 'exp')
- latent_grad: bfloat16 [8, 8, 64, 384], P('section', 'seq', 'exp')
All inputs are finite; a program needn't handle non-finite values.
Results may differ from a plain program's by a relative error of at most 0.015.
Values may be sent and summed in bfloat16 or wider, within the bound.
A program may use at most 64 MiB of HBM per device.

v0:
```python
import jax
import jax.numpy as jnp
from jax import lax
from jax.sharding import PartitionSpec as P

epsilon = 1e-06


def from_behind(shard, axis, by):
    size = lax.axis_size(axis)
    pairs = [(i, i + by) for i in range(size) if 0 <= i + by < size]
    return lax.ppermute(shard, axis, pairs)


def extended_2(block, sides, width):
    for axis, dim in sides:
        count = lax.axis_size(axis)
        forward = [(i, i + 1) for i in range(count - 1)]
        backward = [(target, source) for source, target in forward]
        low = lax.ppermute(
            lax.slice_in_dim(block, block.shape[dim] - width, None, axis=dim), axis, forward
        )
        high = lax.ppermute(lax.slice_in_dim(block, 0, width, axis=dim), axis, backward)
        block = jnp.concatenate([low, block, high], axis=dim)
    return block


def normalize(values, gain):
    inverse = lax.rsqrt(jnp.mean(values * values, axis=-1, keepdims=True) + epsilon)
    return (values * inverse * gain, inverse)


def norm_backward(values, inverse, gain, upstream):
    scaled = upstream * gain
    return inverse * scaled - values * inverse**3 * jnp.mean(
        values * scaled, axis=-1, keepdims=True
    )


def silu_slope(normed):
    sigma = jax.nn.sigmoid(normed)
    return sigma * (1.0 + normed * (1.0 - sigma))


def forward_kernel(weight):
    swapped = jnp.swapaxes(weight, 3, 4)
    return swapped.reshape(3, 3, 3 * swapped.shape[3], swapped.shape[4])


def backward_kernel(weight):
    flipped = weight[::-1, ::-1, ::-1]
    return flipped.reshape(3, 3, 3 * flipped.shape[3], flipped.shape[4])


def conv_taps(padded, kernel, frame_count, row_count, col_count):
    summed = jnp.zeros((frame_count * row_count * col_count, kernel.shape[3]), jnp.float32)
    for time_tap in range(3):
        for row_tap in range(3):
            columns = jnp.concatenate(
                [
                    padded[
                        time_tap : time_tap + frame_count,
                        row_tap : row_tap + row_count,
                        col_tap : col_tap + col_count,
                    ]
                    for col_tap in range(3)
                ],
                axis=-1,
            )
            columns = columns.reshape(frame_count * row_count * col_count, columns.shape[-1])
            summed = summed + jnp.dot(
                columns, kernel[time_tap, row_tap], preferred_element_type=jnp.float32
            )
    return summed.reshape(frame_count, row_count, col_count, kernel.shape[3])


def forward_conv(active, weight):
    frame_count, row_count, col_count = (active.shape[0], active.shape[1], active.shape[2])
    earlier = from_behind(active, "section", 1)
    extended = jnp.concatenate([earlier, active], axis=0)
    bordered = extended_2(extended, (("seq", 1),), 1)
    gathered = lax.all_gather(bordered, "exp", axis=2, tiled=True)
    padded = jnp.pad(gathered, ((0, 0), (0, 0), (1, 1), (0, 0)))
    partial_value = conv_taps(
        padded, forward_kernel(weight), frame_count, row_count, gathered.shape[2]
    )
    return lax.all_to_all(
        partial_value.astype(jnp.bfloat16), "exp", split_axis=2, concat_axis=3, tiled=True
    ).astype(partial_value.dtype)


def backward_conv(upstream, weight):
    frame_count, row_count, col_count = (upstream.shape[0], upstream.shape[1], upstream.shape[2])
    following = from_behind(upstream, "section", -1)
    extended = jnp.concatenate([upstream, following], axis=0)
    regrouped = lax.all_to_all(extended, "exp", split_axis=3, concat_axis=2, tiled=True)
    bordered = extended_2(regrouped, (("seq", 1),), 1)
    padded = jnp.pad(bordered, ((0, 0), (0, 0), (1, 1), (0, 0)))
    partial_value = conv_taps(
        padded, backward_kernel(weight), frame_count, row_count, regrouped.shape[2]
    )
    return lax.psum_scatter(
        partial_value.astype(jnp.bfloat16), "exp", scatter_dimension=2, tiled=True
    ).astype(jnp.float32)


def body(latent, cotangent, gain_one, gain_two, kernel_one, kernel_two):
    weight_one, weight_two = (kernel_one, kernel_two)
    source = latent.astype(jnp.float32)
    normed_one, inverse_one = normalize(source, gain_one)
    active_one = jax.nn.silu(normed_one).astype(jnp.bfloat16)
    inner = forward_conv(active_one, weight_one)
    normed_two, inverse_two = normalize(inner, gain_two)
    active_two = jax.nn.silu(normed_two).astype(jnp.bfloat16)
    branch = forward_conv(active_two, weight_two)
    block_out = (source + branch).astype(jnp.bfloat16)
    grad_two = backward_conv(cotangent, weight_two)
    grad_inner = norm_backward(
        inner, inverse_two, gain_two, grad_two * silu_slope(normed_two)
    ).astype(jnp.bfloat16)
    grad_one = backward_conv(grad_inner, weight_one)
    latent_grad = cotangent.astype(jnp.float32) + norm_backward(
        source, inverse_one, gain_one, grad_one * silu_slope(normed_one)
    )
    return (block_out, latent_grad.astype(jnp.bfloat16))


def solution(mesh):
    in_specs = (
        P("section", "seq", "exp", None),
        P("section", "seq", "exp", None),
        P(),
        P(),
        P(None, None, None, "exp", None),
        P(None, None, None, "exp", None),
    )
    out_specs = (P("section", "seq", "exp", None), P("section", "seq", "exp", None))
    return jax.shard_map(body, mesh=mesh, in_specs=in_specs, out_specs=out_specs, check_vma=False)
```

profile of v0, /device:TPU:0, one launch (start us, length us, event | category | flops | bytes accessed | tf_op | source)
XLA Modules:
  0.0 215.2 jit_solution(15141144840424351052)
XLA Ops:
  10.5 5.5 %collective-permute-start = (bf16[2,4,16,384]{3,2,1,0:T(8,128)(2,1)S(1)}, bf16[2,4,16,384]{3,2,1,0:T(8,128)(2,1)S(1)}, u32[]{:S(2)}, u32[]{:S(2)}) collective-permute-start(bf16[2,4,16,384]{3,2,1,0:T(8,128)(2,1)S(1)} %fusion.60), channel_id=1, source_target_pairs={{0,8},{8,16},{16,24},{1,9},{9,17},{17,25},{2,10},{10,18},{18,26},{... | collective-permute-start | bytes 294920 | tf_op jit(solution)/shard_map/ppermute | solution.py:12
  17.0 2.4 %copy.83 = bf16[4,4,16,384]{2,1,0,3:T(4,128)(2,1)} copy(bf16[4,4,16,384]{3,2,1,0:T(8,128)(2,1)S(1)} %pad_maximum_fusion.32) | data formatting | bytes 393216 | tf_op jit(solution)/shard_map/concatenate | solution.py:95
  19.4 4.0 %reshape.237 = bf16[4,2,12288]{2,1,0:T(2,128)(2,1)} reshape(bf16[384,4,4,16]{3,2,1,0:T(4,128)(2,1)} %bitcast.261) | data formatting | bytes 393216
  23.4 5.4 %all-to-all-start.2 = ((bf16[4,2,12288]{2,1,0:T(2,128)(2,1)}), bf16[4,2,12288]{2,1,0:T(2,128)(2,1)S(1)}, u32[]{:S(2)}, u32[]{:S(2)}) async-start(bf16[4,2,12288]{2,1,0:T(2,128)(2,1)} %reshape.237), calls=%async_computation.2 | async-start | bytes 393216 | tf_op jit(solution)/shard_map/all_to_all | solution.py:96
  30.2 3.0 %collective-permute-start.1 = (bf16[4,1,16,384]{3,2,1,0:T(8,128)(2,1)S(1)}, bf16[4,1,16,384]{3,2,1,0:T(8,128)(2,1)S(1)}, u32[]{:S(2)}, u32[]{:S(2)}) collective-permute-start(bf16[4,1,16,384]{3,2,1,0:T(8,128)(2,1)S(1)} %get-tuple-element.122), channel_id=1, source_target_pairs={{0,4},{1,5},{2,6},{3,7},{8,12},{9,13},{10,14},{11,15},{16,20},{17,... | collective-permute-start | bytes 147464 | tf_op jit(solution)/shard_map/ppermute | solution.py:20
  33.2 1.5 copy.99
  34.7 3.0 %rev.6 = bf16[3,3,3,96,384]{4,3,2,1,0:T(8,128)(2,1)} reverse(bf16[3,3,3,96,384]{4,3,2,1,0:T(8,128)(2,1)} %param.11), dimensions={0,1,2} | reverse | bytes 3981312 | tf_op jit(solution)/shard_map/rev | solution.py:51
  39.8 1.4 copy.85
  42.6 3.2 %collective-permute-start.7 = (bf16[4,1,64,96]{3,2,1,0:T(8,128)(2,1)S(1)}, bf16[4,1,64,96]{3,2,1,0:T(8,128)(2,1)S(1)}, u32[]{:S(2)}, u32[]{:S(2)}) collective-permute-start(bf16[4,1,64,96]{3,2,1,0:T(8,128)(2,1)S(1)} %get-tuple-element.116), channel_id=1, source_target_pairs={{0,4},{1,5},{2,6},{3,7},{8,12},{9,13},{10,14},{11,15},{16,20},{17,... | collective-permute-start | bytes 147464 | tf_op jit(solution)/shard_map/ppermute | solution.py:20
  45.8 1.5 copy.95
  55.0 15.4 %all-gather.3.cloned.1.call-done = bf16[4,6,64,384]{3,2,1,0:T(8,128)(2,1)} async-done(((bf16[4,6,16,384]{3,2,1,0:T(8,128)(2,1)}), bf16[4,6,64,384]{3,2,1,0:T(8,128)(2,1)}) %all-gather.3.cloned.1.call-update) | async-done | bytes 1179664 | tf_op jit(solution)/shard_map/all_gather | solution.py:82
  70.4 4.1 %pad_slice_fusion.35 = (bf16[2,4,64,384]{3,2,1,0:T(8,128)(2,1)S(1)}, bf16[2,4,64,384]{3,2,1,0:T(8,128)(2,1)S(1)}, bf16[2,4,64,384]{3,2,1,0:T(8,128)(2,1)S(1)}, b...) fusion(bf16[4,6,64,384]{3,2,1,0:T(8,128)(2,1)} %all-gather.3.cl, ...), kind=kLoop, calls=%fused_computation.250 | loop fusion | bytes 5505024 | tf_op jit(solution)/shard_map/slice | solution.py:61
  82.9 9.2 %all_to_all.54 = bf16[2,4,64,96]{3,1,0,2:T(4,128)(2,1)S(1)} all-to-all(bf16[2,4,64,96]{3,1,0,2:T(4,128)(2,1)S(1)} %copy.75), channel_id=1, replica_groups=mesh['section'=4,'seq'=2,'exp'=4] {'exp'}, dimensions={2} | all-to-all | bytes 196608 | tf_op jit(solution)/shard_map/all_to_all | solution.py:87
  96.6 5.2 %collective-permute-done.9 = bf16[2,4,16,384]{3,2,1,0:T(8,128)(2,1)S(1)} collective-permute-done((bf16[2,4,16,384]{3,2,1,0:T(8,128)(2,1)S(1)}, bf16[2,4,16,384]{3,2,1,0:T(8,128)(2,1)S(1)}, u32[]{:S(2)}, u32[]{:S(2)}) %collective-permute-start.9) | collective-permute-done | bytes 98336 | tf_op jit(solution)/shard_map/ppermute | solution.py:12
  101.9 2.4 %copy.89 = bf16[4,4,16,384]{2,1,0,3:T(4,128)(2,1)} copy(bf16[4,4,16,384]{3,2,1,0:T(8,128)(2,1)S(1)} %pad_maximum_fusion.33) | data formatting | bytes 393216 | tf_op jit(solution)/shard_map/concatenate | solution.py:95
  104.3 4.0 %reshape.239 = bf16[4,2,12288]{2,1,0:T(2,128)(2,1)} reshape(bf16[384,4,4,16]{3,2,1,0:T(4,128)(2,1)} %bitcast.262) | data formatting | bytes 393216
  108.3 3.4 %all-to-all-start.3 = ((bf16[4,2,12288]{2,1,0:T(2,128)(2,1)}), bf16[4,2,12288]{2,1,0:T(2,128)(2,1)S(1)}, u32[]{:S(2)}, u32[]{:S(2)}) async-start(bf16[4,2,12288]{2,1,0:T(2,128)(2,1)} %reshape.239), calls=%async_computation.4 | async-start | bytes 393216 | tf_op jit(solution)/shard_map/all_to_all | solution.py:96
  111.8 1.5 rev.7
  113.3 4.6 %all-to-all-done.3 = bf16[4,2,12288]{2,1,0:T(2,128)(2,1)S(1)} async-done(((bf16[4,2,12288]{2,1,0:T(2,128)(2,1)}), bf16[4,2,12288]{2,1,0:T(2,128)(2,1)S(1)}, u32[]{:S(2)}, u32[]{:S(2)}) %all-to-all-start.3) | async-done | bytes 196640 | tf_op jit(solution)/shard_map/all_to_all | solution.py:96
  119.1 1.4 copy.91
  121.8 3.0 %collective-permute-start.10 = (bf16[4,1,64,96]{3,2,1,0:T(8,128)(2,1)S(1)}, bf16[4,1,64,96]{3,2,1,0:T(8,128)(2,1)S(1)}, u32[]{:S(2)}, u32[]{:S(2)}) collective-permute-start(bf16[4,1,64,96]{3,2,1,0:T(8,128)(2,1)S(1)} %get-tuple-element.107), channel_id=1, source_target_pairs={{0,4},{1,5},{2,6},{3,7},{8,12},{9,13},{10,14},{11,15},{16,20},{17,... | collective-permute-start | bytes 147464 | tf_op jit(solution)/shard_map/ppermute | solution.py:20
  124.9 1.5 copy.97
  134.1 4.5 %collective-permute-start.3 = (bf16[2,4,16,384]{3,2,1,0:T(8,128)(2,1)S(1)}, bf16[2,4,16,384]{3,2,1,0:T(8,128)(2,1)S(1)}, u32[]{:S(2)}, u32[]{:S(2)}) collective-permute-start(bf16[2,4,16,384]{3,2,1,0:T(8,128)(2,1)S(1)} %get-tuple-element.119), channel_id=1, source_target_pairs={{0,8},{8,16},{16,24},{1,9},{9,17},{17,25},{2,10},{10,18},{18,26},{... | collective-permute-start | bytes 294920 | tf_op jit(solution)/shard_map/ppermute | solution.py:12
  138.6 2.2 %collective-permute-done.3 = bf16[2,4,16,384]{3,2,1,0:T(8,128)(2,1)S(1)} collective-permute-done((bf16[2,4,16,384]{3,2,1,0:T(8,128)(2,1)S(1)}, bf16[2,4,16,384]{3,2,1,0:T(8,128)(2,1)S(1)}, u32[]{:S(2)}, u32[]{:S(2)}) %collective-permute-start.3) | collective-permute-done | bytes 98336 | tf_op jit(solution)/shard_map/ppermute | solution.py:12
  142.1 3.3 %collective-permute-start.4 = (bf16[4,1,16,384]{3,2,1,0:T(8,128)(2,1)S(1)}, bf16[4,1,16,384]{3,2,1,0:T(8,128)(2,1)S(1)}, u32[]{:S(2)}, u32[]{:S(2)}) collective-permute-start(bf16[4,1,16,384]{3,2,1,0:T(8,128)(2,1)S(1)} %get-tuple-element.120), channel_id=1, source_target_pairs={{0,4},{1,5},{2,6},{3,7},{8,12},{9,13},{10,14},{11,15},{16,20},{17,... | collective-permute-start | bytes 147464 | tf_op jit(solution)/shard_map/ppermute | solution.py:20
  146.9 1.5 copy.100
  148.3 6.4 %reduce-scatter.5.cloned.1.call-done = bf16[2,4,16,384]{3,2,1,0:T(8,128)(2,1)} async-done(((bf16[2,4,64,384]{3,2,1,0:T(8,128)(2,1)}), bf16[2,4,16,384]{3,2,1,0:T(8,128)(2,1)}) %reduce-scatter.5.cloned.1.call-update) | async-done | bytes 98320 | tf_op jit(solution)/shard_map/reduce_scatter | solution.py:102
  155.9 28.8 %all-gather.5.cloned.1.call-done = bf16[4,6,64,384]{3,2,1,0:T(8,128)(2,1)} async-done(((bf16[4,6,16,384]{3,2,1,0:T(8,128)(2,1)}), bf16[4,6,64,384]{3,2,1,0:T(8,128)(2,1)}) %all-gather.5.cloned.1.call-update) | async-done | bytes 1179664 | tf_op jit(solution)/shard_map/all_gather | solution.py:82
  184.7 4.1 %pad_slice_fusion.17 = (bf16[2,4,64,384]{3,2,1,0:T(8,128)(2,1)S(1)}, bf16[2,4,64,384]{3,2,1,0:T(8,128)(2,1)S(1)}, bf16[2,4,64,384]{3,2,1,0:T(8,128)(2,1)S(1)}, b...) fusion(bf16[4,6,64,384]{3,2,1,0:T(8,128)(2,1)} %all-gather.5.cl, ...), kind=kLoop, calls=%fused_computation.232 | loop fusion | bytes 5505024 | tf_op jit(solution)/shard_map/slice | solution.py:61
  189.4 1.4 copy-done.8
  198.2 3.3 %all-to-all-start.1 = ((bf16[2,4,64,96]{3,1,0,2:T(4,128)(2,1)}), bf16[2,4,64,96]{3,1,0,2:T(4,128)(2,1)S(1)}, u32[]{:S(2)}, u32[]{:S(2)}) async-start(bf16[2,4,64,96]{3,1,0,2:T(4,128)(2,1)} %copy.80), calls=%async_computation.1 | async-start | bytes 262144 | tf_op jit(solution)/shard_map/all_to_all | solution.py:87
  201.5 5.9 %all-to-all-done.1 = bf16[2,4,64,96]{3,1,0,2:T(4,128)(2,1)S(1)} async-done(((bf16[2,4,64,96]{3,1,0,2:T(4,128)(2,1)}), bf16[2,4,64,96]{3,1,0,2:T(4,128)(2,1)S(1)}, u32[]{:S(2)}, u32[]{:S(2)}) %all-to-all-start.1) | async-done | bytes 98336 | tf_op jit(solution)/shard_map/all_to_all | solution.py:87
  (163 shorter events, 52.0 us)
Async XLA Ops:
  7.2 8.9 %collective-permute-start.6 = (bf16[2,4,16,384]{3,2,1,0:T(8,128)(2,1)}, bf16[2,4,16,384]{3,2,1,0:T(8,128)(2,1)S(1)}, u32[]{:S(2)}, u32[]{:S(2)}) collective-permute-start(bf16[2,4,16,384]{3,2,1,0:T(8,128)(2,1)} %param.7), channel_id=1, source_target_pairs={{8,0},{16,8},{24,16},{9,1},{17,9},{25,17},{10,2},{18,10},{26,18},{... | collective-permute-start | bytes 294920 | tf_op jit(solution)/shard_map/ppermute | solution.py:12
  10.5 18.3 %collective-permute-start = (bf16[2,4,16,384]{3,2,1,0:T(8,128)(2,1)S(1)}, bf16[2,4,16,384]{3,2,1,0:T(8,128)(2,1)S(1)}, u32[]{:S(2)}, u32[]{:S(2)}) collective-permute-start(bf16[2,4,16,384]{3,2,1,0:T(8,128)(2,1)S(1)} %fusion.60), channel_id=1, source_target_pairs={{0,8},{8,16},{16,24},{1,9},{9,17},{17,25},{2,10},{10,18},{18,26},{... | collective-permute-start | bytes 294920 | tf_op jit(solution)/shard_map/ppermute | solution.py:12
  19.4 13.8 %copy-start.4 = (bf16[3,3,3,96,384]{4,3,2,1,0:T(8,128)(2,1)S(1)}, bf16[3,3,3,96,384]{4,3,2,1,0:T(8,128)(2,1)}, u32[]{:S(2)}) copy-start(bf16[3,3,3,96,384]{4,3,2,1,0:T(8,128)(2,1)} %param.10) | copy-start | bytes 5971972
  23.4 15.2 %all-to-all-start.2 = ((bf16[4,2,12288]{2,1,0:T(2,128)(2,1)}), bf16[4,2,12288]{2,1,0:T(2,128)(2,1)S(1)}, u32[]{:S(2)}, u32[]{:S(2)}) async-start(bf16[4,2,12288]{2,1,0:T(2,128)(2,1)} %reshape.237), calls=%async_computation.2 | async-start | bytes 393216 | tf_op jit(solution)/shard_map/all_to_all | solution.py:96
  28.8 41.6 %all-gather.3.cloned.1.call-start = ((), (), s32[]{:S(2)}) async-start(), calls=%async_computation.6 | async-start | bytes 1474560 | tf_op jit(solution)/shard_map/all_gather | solution.py:82
  28.9 8.9 %collective-permute-start.2 = (bf16[4,1,16,384]{3,2,1,0:T(8,128)(2,1)S(1)}, bf16[4,1,16,384]{3,2,1,0:T(8,128)(2,1)S(1)}, u32[]{:S(2)}, u32[]{:S(2)}) collective-permute-start(bf16[4,1,16,384]{3,2,1,0:T(8,128)(2,1)S(1)} %get-tuple-element.123), channel_id=1, source_target_pairs={{4,0},{5,1},{6,2},{7,3},{12,8},{13,9},{14,10},{15,11},{20,16},{21,... | collective-permute-start | bytes 147464 | tf_op jit(solution)/shard_map/ppermute | solution.py:23
  30.2 7.6 %collective-permute-start.1 = (bf16[4,1,16,384]{3,2,1,0:T(8,128)(2,1)S(1)}, bf16[4,1,16,384]{3,2,1,0:T(8,128)(2,1)S(1)}, u32[]{:S(2)}, u32[]{:S(2)}) collective-permute-start(bf16[4,1,16,384]{3,2,1,0:T(8,128)(2,1)S(1)} %get-tuple-element.122), channel_id=1, source_target_pairs={{0,4},{1,5},{2,6},{3,7},{8,12},{9,13},{10,14},{11,15},{16,20},{17,... | collective-permute-start | bytes 147464 | tf_op jit(solution)/shard_map/ppermute | solution.py:20
  38.6 54.5 %reduce-scatter.3.cloned.1.call-start = ((), (), s32[]{:S(2)}) async-start(), calls=%async_computation.8 | async-start | bytes 491520 | tf_op jit(solution)/shard_map/reduce_scatter | solution.py:102
  41.3 6.3 %collective-permute-start.8 = (bf16[4,1,64,96]{3,2,1,0:T(8,128)(2,1)S(1)}, bf16[4,1,64,96]{3,2,1,0:T(8,128)(2,1)S(1)}, u32[]{:S(2)}, u32[]{:S(2)}) collective-permute-start(bf16[4,1,64,96]{3,2,1,0:T(8,128)(2,1)S(1)} %get-tuple-element.117), channel_id=1, source_target_pairs={{4,0},{5,1},{6,2},{7,3},{12,8},{13,9},{14,10},{15,11},{20,16},{21,... | collective-permute-start | bytes 147464 | tf_op jit(solution)/shard_map/ppermute | solution.py:23
  42.6 5.0 %collective-permute-start.7 = (bf16[4,1,64,96]{3,2,1,0:T(8,128)(2,1)S(1)}, bf16[4,1,64,96]{3,2,1,0:T(8,128)(2,1)S(1)}, u32[]{:S(2)}, u32[]{:S(2)}) collective-permute-start(bf16[4,1,64,96]{3,2,1,0:T(8,128)(2,1)S(1)} %get-tuple-element.116), channel_id=1, source_target_pairs={{0,4},{1,5},{2,6},{3,7},{8,12},{9,13},{10,14},{11,15},{16,20},{17,... | collective-permute-start | bytes 147464 | tf_op jit(solution)/shard_map/ppermute | solution.py:20
  48.3 1.6 copy-start.2
  70.4 4.1 %copy-start = (bf16[4,6,64,384]{3,2,1,0:T(8,128)(2,1)S(1)}, bf16[4,6,64,384]{3,2,1,0:T(8,128)(2,1)}, u32[]{:S(2)}) copy-start(bf16[4,6,64,384]{3,2,1,0:T(8,128)(2,1)} %all-gather.3.cloned.1.call-done) | copy-start | bytes 3538948
  74.9 1.6 copy-start.7
  82.7 10.4 %copy-start.13 = (f32[384]{0:T(512)S(1)}, f32[384]{0:T(512)}, u32[]{:S(2)}) copy-start(f32[384]{0:T(512)} %param.9) | copy-start | bytes 4612
  95.3 6.5 %collective-permute-start.9 = (bf16[2,4,16,384]{3,2,1,0:T(8,128)(2,1)S(1)}, bf16[2,4,16,384]{3,2,1,0:T(8,128)(2,1)S(1)}, u32[]{:S(2)}, u32[]{:S(2)}) collective-permute-start(bf16[2,4,16,384]{3,2,1,0:T(8,128)(2,1)S(1)} %get-tuple-element.118), channel_id=1, source_target_pairs={{8,0},{16,8},{24,16},{9,1},{17,9},{25,17},{10,2},{18,10},{26,18},{... | collective-permute-start | bytes 294920 | tf_op jit(solution)/shard_map/ppermute | solution.py:12
  104.3 7.5 %copy-start.5 = (bf16[3,3,3,96,384]{4,3,2,1,0:T(8,128)(2,1)S(1)}, bf16[3,3,3,96,384]{4,3,2,1,0:T(8,128)(2,1)}, u32[]{:S(2)}) copy-start(bf16[3,3,3,96,384]{4,3,2,1,0:T(8,128)(2,1)} %param.10) | copy-start | bytes 5971972
  108.3 9.6 %all-to-all-start.3 = ((bf16[4,2,12288]{2,1,0:T(2,128)(2,1)}), bf16[4,2,12288]{2,1,0:T(2,128)(2,1)S(1)}, u32[]{:S(2)}, u32[]{:S(2)}) async-start(bf16[4,2,12288]{2,1,0:T(2,128)(2,1)} %reshape.239), calls=%async_computation.4 | async-start | bytes 393216 | tf_op jit(solution)/shard_map/all_to_all | solution.py:96
  111.7 43.0 %reduce-scatter.5.cloned.1.call-start = ((), (), s32[]{:S(2)}) async-start(), calls=%async_computation.9 | async-start | bytes 491520 | tf_op jit(solution)/shard_map/reduce_scatter | solution.py:102
  120.5 6.1 %collective-permute-start.11 = (bf16[4,1,64,96]{3,2,1,0:T(8,128)(2,1)S(1)}, bf16[4,1,64,96]{3,2,1,0:T(8,128)(2,1)S(1)}, u32[]{:S(2)}, u32[]{:S(2)}) collective-permute-start(bf16[4,1,64,96]{3,2,1,0:T(8,128)(2,1)S(1)} %get-tuple-element.108), channel_id=1, source_target_pairs={{4,0},{5,1},{6,2},{7,3},{12,8},{13,9},{14,10},{15,11},{20,16},{21,... | collective-permute-start | bytes 147464 | tf_op jit(solution)/shard_map/ppermute | solution.py:23
  121.8 4.8 %collective-permute-start.10 = (bf16[4,1,64,96]{3,2,1,0:T(8,128)(2,1)S(1)}, bf16[4,1,64,96]{3,2,1,0:T(8,128)(2,1)S(1)}, u32[]{:S(2)}, u32[]{:S(2)}) collective-permute-start(bf16[4,1,64,96]{3,2,1,0:T(8,128)(2,1)S(1)} %get-tuple-element.107), channel_id=1, source_target_pairs={{0,4},{1,5},{2,6},{3,7},{8,12},{9,13},{10,14},{11,15},{16,20},{17,... | collective-permute-start | bytes 147464 | tf_op jit(solution)/shard_map/ppermute | solution.py:20
  126.8 1.6 copy-start.3
  132.8 14.0 %copy-start.6 = (bf16[3,3,3,96,384]{4,3,2,1,0:T(8,128)(2,1)S(1)}, bf16[3,3,3,96,384]{4,3,2,1,0:T(8,128)(2,1)}, u32[]{:S(2)}) copy-start(bf16[3,3,3,96,384]{4,3,2,1,0:T(8,128)(2,1)} %param.11) | copy-start | bytes 5971972
  134.0 50.7 %all-gather.5.cloned.1.call-start = ((), (), s32[]{:S(2)}) async-start(), calls=%async_computation.7 | async-start | bytes 1474560 | tf_op jit(solution)/shard_map/all_gather | solution.py:82
  134.1 6.7 %collective-permute-start.3 = (bf16[2,4,16,384]{3,2,1,0:T(8,128)(2,1)S(1)}, bf16[2,4,16,384]{3,2,1,0:T(8,128)(2,1)S(1)}, u32[]{:S(2)}, u32[]{:S(2)}) collective-permute-start(bf16[2,4,16,384]{3,2,1,0:T(8,128)(2,1)S(1)} %get-tuple-element.119), channel_id=1, source_target_pairs={{0,8},{8,16},{16,24},{1,9},{9,17},{17,25},{2,10},{10,18},{18,26},{... | collective-permute-start | bytes 294920 | tf_op jit(solution)/shard_map/ppermute | solution.py:12
  140.8 4.6 %collective-permute-start.5 = (bf16[4,1,16,384]{3,2,1,0:T(8,128)(2,1)S(1)}, bf16[4,1,16,384]{3,2,1,0:T(8,128)(2,1)S(1)}, u32[]{:S(2)}, u32[]{:S(2)}) collective-permute-start(bf16[4,1,16,384]{3,2,1,0:T(8,128)(2,1)S(1)} %get-tuple-element.121), channel_id=1, source_target_pairs={{4,0},{5,1},{6,2},{7,3},{12,8},{13,9},{14,10},{15,11},{20,16},{21,... | collective-permute-start | bytes 147464 | tf_op jit(solution)/shard_map/ppermute | solution.py:23
  142.1 3.9 %collective-permute-start.4 = (bf16[4,1,16,384]{3,2,1,0:T(8,128)(2,1)S(1)}, bf16[4,1,16,384]{3,2,1,0:T(8,128)(2,1)S(1)}, u32[]{:S(2)}, u32[]{:S(2)}) collective-permute-start(bf16[4,1,16,384]{3,2,1,0:T(8,128)(2,1)S(1)} %get-tuple-element.120), channel_id=1, source_target_pairs={{0,4},{1,5},{2,6},{3,7},{8,12},{9,13},{10,14},{11,15},{16,20},{17,... | collective-permute-start | bytes 147464 | tf_op jit(solution)/shard_map/ppermute | solution.py:20
  146.8 7.9 %copy-start.9 = (bf16[2,4,16,384]{3,2,1,0:T(8,128)(2,1)S(1)}, bf16[2,4,16,384]{3,2,1,0:T(8,128)(2,1)}, u32[]{:S(2)}) copy-start(bf16[2,4,16,384]{3,2,1,0:T(8,128)(2,1)} %param.6) | copy-start | bytes 294916
  146.8 7.9 %copy-start.12 = (f32[384]{0:T(512)S(1)}, f32[384]{0:T(512)}, u32[]{:S(2)}) copy-start(f32[384]{0:T(512)} %param.8) | copy-start | bytes 4612
  184.7 4.1 %copy-start.1 = (bf16[4,6,64,384]{3,2,1,0:T(8,128)(2,1)S(1)}, bf16[4,6,64,384]{3,2,1,0:T(8,128)(2,1)}, u32[]{:S(2)}) copy-start(bf16[4,6,64,384]{3,2,1,0:T(8,128)(2,1)} %all-gather.5.cloned.1.call-done) | copy-start | bytes 3538948
  197.3 10.5 %copy-start.10 = (bf16[2,4,16,384]{3,2,1,0:T(8,128)(2,1)S(1)}, bf16[2,4,16,384]{3,2,1,0:T(8,128)(2,1)}, u32[]{:S(2)}) copy-start(bf16[2,4,16,384]{3,2,1,0:T(8,128)(2,1)} %reduce-scatter.5.cloned.1.call-done) | copy-start | bytes 294916
  197.3 10.5 %copy-start.11 = (bf16[2,4,16,384]{3,2,1,0:T(8,128)(2,1)S(1)}, bf16[2,4,16,384]{3,2,1,0:T(8,128)(2,1)}, u32[]{:S(2)}) copy-start(bf16[2,4,16,384]{3,2,1,0:T(8,128)(2,1)} %param.7) | copy-start | bytes 294916
  198.2 9.2 %all-to-all-start.1 = ((bf16[2,4,64,96]{3,1,0,2:T(4,128)(2,1)}), bf16[2,4,64,96]{3,1,0,2:T(4,128)(2,1)S(1)}, u32[]{:S(2)}, u32[]{:S(2)}) async-start(bf16[2,4,64,96]{3,1,0,2:T(4,128)(2,1)} %copy.80), calls=%async_computation.1 | async-start | bytes 262144 | tf_op jit(solution)/shard_map/all_to_all | solution.py:87
  (1 other events, 1.6 us)
Sparse Core Ops, SparseCore 0:
  38.7 31.6 all-gather.2
  72.7 20.3 reduce-scatter.2
  134.1 20.5 reduce-scatter.4
  156.2 28.5 all-gather.4
where the time goes:
time: 216 us; the launch traced here: 215 us
  waiting for transfers between devices  69.5 us (32%)
  local copies, waits for them, and re-layouts  46.8 us (22%)
  starting transfers between devices  42.6 us (20%)
  matrix products  17.7 us (8%)
  between operations  14.7 us (7%)
  other arithmetic  14.5 us (7%)
  blocking collectives  9.24 us (4%)
    all_gather x2, waiting for transfers between devices, forward_conv(): gathered = lax.all_gather(bordered, 'exp', axis=2, tiled=True)  44.3 us
    dot_general x36, matrix products, conv_taps(): jnp.dot(columns, kernel[time_tap, row_tap], preferred_element_type=jnp.fl...  17.7 us
    unnamed x32, local copies, waits for them, and re-layouts  14.8 us
    ppermute x4, starting transfers between devices, from_behind(): return lax.ppermute(shard, axis, pairs)  12.6 us
    ppermute x4, starting transfers between devices, extended_2(): lax.ppermute(lax.slice_in_dim(block, block.shape[dim] - width, None, axis...  12.6 us
    slice x16, local copies, waits for them, and re-layouts, conv_taps(): padded[time_tap:time_tap + frame_count, row_tap:row_tap + row_count, col_...  11.9 us
    all_to_all x1, blocking collectives, forward_conv(): lax.all_to_all(partial_value.astype(jnp.bfloat16), 'exp', split_axis=2, c...  9.24 us
    all_to_all x2, starting transfers between devices, backward_conv(): lax.all_to_all(extended, 'exp', split_axis=3, concat_axis=2, tiled=True)  8.76 us
  transfers between devices with their start and end apart: 19, of which 9 were waited for; matrix products, arithmetic and copies ran while one was open for 20% of the time, Pallas kernels for 0%

commit v1 on v0

v1 whole, which is shorter than its diff:
```python
import functools

import jax
import jax.numpy as jnp
from jax import lax
from jax.experimental import pallas as pl
from jax.experimental.pallas import tpu as pltpu
from jax.sharding import PartitionSpec as P

epsilon = 1e-06
MESH = pl.DeviceIdType.MESH
bf16, f32 = jnp.bfloat16, jnp.float32


def normalize(values, gain):
    inverse = lax.rsqrt(jnp.mean(values * values, axis=-1, keepdims=True) + epsilon)
    return values * inverse * gain, inverse


def norm_backward(values, inverse, gain, upstream):
    scaled = upstream * gain
    mean = jnp.mean(values * scaled, axis=-1, keepdims=True)
    return inverse * scaled - values * (inverse * inverse * inverse) * mean


def silu(normed):
    return normed / (1.0 + jnp.exp(-normed))


def silu_slope(normed):
    sigma = 1.0 / (1.0 + jnp.exp(-normed))
    return sigma * (1.0 + normed * (1.0 - sigma))


def shift_sum(taps, width, size):
    rows = taps.shape[0]
    column = lax.rem(lax.broadcasted_iota(jnp.int32, (rows, size), 0), width)
    low = pltpu.roll(taps[:, :size], 1, axis=0)
    high = pltpu.roll(taps[:, 2 * size :], rows - 1, axis=0)
    return (
        taps[:, size : 2 * size]
        + jnp.where(column == 0, 0.0, low)
        + jnp.where(column == width - 1, 0.0, high)
    )


def stage(index, sizes, act, grad, w_fwd, w_bwd, bufs, send, recv, w_ready):
    S, Q, Z = sizes
    xp, qs, qp, yf, rf, rp, yb, rb = bufs
    F, R, W, C = act.shape
    O = w_fwd.shape[3]
    WW = W * Z
    OP = -(-O // 128) * 128
    s, q, z = lax.axis_index("section"), lax.axis_index("seq"), lax.axis_index("exp")
    has_next, has_prev = s < S - 1, s > 0
    has_high, has_low = q < Q - 1, q > 0
    nxt, prv = jnp.minimum(s + 1, S - 1), jnp.maximum(s - 1, 0)
    upper, lower = jnp.minimum(q + 1, Q - 1), jnp.maximum(q - 1, 0)
    mine = pl.ds(pl.multiple_of(z * W, W), W)
    body = pl.ds(1, R)

    def peer(d):
        return lax.rem(z + d, Z)

    def columns(d):
        return pl.ds(pl.multiple_of(peer(d) * W, W), W)

    def remote(src, dst, slot, device):
        return pltpu.make_async_remote_copy(
            src_ref=src,
            dst_ref=dst,
            send_sem=send.at[index, slot],
            recv_sem=recv.at[index, slot],
            device_id=device,
            device_id_type=MESH,
        )

    def q_own(d):
        return remote(qs.at[peer(d)], qp.at[pl.ds(0, F), body, mine], d, (s, q, peer(d)))

    def q_prev(d):
        return remote(
            qs.at[peer(d), pl.ds(0, 2)], qp.at[pl.ds(F, 2), body, mine], Z + d, (prv, q, peer(d))
        )

    def x_own(d):
        return remote(act, xp.at[:, body, mine], 2 * Z + d, (s, q, peer(d)))

    def b_own(d):
        return remote(yb.at[:, :, columns(d)], rb.at[d], 3 * Z + d, (s, q, peer(d)))

    def f_own(d):
        return remote(
            yf.at[pl.ds(0, F), :, columns(d)], rf.at[z], 4 * Z + d, (s, q, peer(d))
        )

    def f_next(d):
        return remote(
            yf.at[pl.ds(F, 2), :, columns(d)], rp.at[z], 5 * Z + d, (nxt, q, peer(d))
        )

    def to_high(buf, slot):
        return remote(buf.at[:, R], buf.at[:, 0], slot, (s, upper, z))

    def to_low(buf, slot):
        return remote(buf.at[:, 1], buf.at[:, R + 1], slot, (s, lower, z))

    def exchange_rows(buf, slot):
        @pl.when(has_high)
        def _():
            to_high(buf, slot).start()

        @pl.when(has_low)
        def _():
            to_low(buf, slot + 1).start()

        @pl.when(jnp.logical_not(has_low))
        def _():
            buf[:, 0] = jnp.zeros_like(buf[:, 0])

        @pl.when(jnp.logical_not(has_high))
        def _():
            buf[:, R + 1] = jnp.zeros_like(buf[:, R + 1])

        @pl.when(has_low)
        def _():
            to_high(buf, slot).wait_recv()

        @pl.when(has_high)
        def _():
            to_low(buf, slot + 1).wait_recv()

    for m in range(Z):
        qs[m] = grad[:, :, :, m * O : (m + 1) * O]
    for d in range(1, Z):
        q_own(d).start()

    @pl.when(has_prev)
    def _():
        for d in range(Z):
            q_prev(d).start()

    for d in range(1, Z):
        x_own(d).start()
    qp[pl.ds(0, F), body, mine] = qs[z]
    xp[:, body, mine] = act[...]

    @pl.when(jnp.logical_not(has_next))
    def _():
        qp[pl.ds(F, 2), body] = jnp.zeros((2, R, WW, O), bf16)

    for d in range(1, Z):
        q_own(d).wait_recv()

    @pl.when(has_next)
    def _():
        for d in range(Z):
            q_prev(d).wait_recv()

    exchange_rows(qp, 6 * Z)
    w_ready[1].wait()

    def padded(value, axis):
        shape = list(value.shape)
        shape[axis] = OP - O
        if OP == O:
            return value
        return jnp.concatenate([value, jnp.zeros(shape, value.dtype)], axis=axis)

    for f in range(F):
        total = None
        for i in range(3):
            lhs = jnp.concatenate(
                [padded(qp[f + i, pl.ds(j, R)].reshape(R * WW, O), 1) for j in range(3)], axis=1
            )
            rhs = jnp.concatenate(
                [
                    jnp.concatenate(
                        [padded(w_bwd[2 - i, 2 - j, 2 - l], 0) for l in range(3)], axis=1
                    )
                    for j in range(3)
                ],
                axis=0,
            )
            part = jnp.dot(lhs, rhs, preferred_element_type=f32)
            total = part if total is None else total + part
        yb[f] = shift_sum(total, WW, C).astype(bf16).reshape(R, WW, C)
    for d in range(1, Z):
        b_own(d).start()

    for d in range(1, Z):
        x_own(d).wait_recv()
    exchange_rows(xp, 6 * Z + 2)
    w_ready[0].wait()
    for t in list(range(F, F + 2)) + list(range(F)):
        total = None
        for i in range(3):
            f = t + i - 2
            if not 0 <= f < F:
                continue
            lhs = jnp.concatenate(
                [xp[f, pl.ds(j, R)].reshape(R * WW, C) for j in range(3)], axis=1
            )
            rhs = jnp.concatenate(
                [
                    jnp.concatenate([padded(w_fwd[i, j, l], 0) for l in range(3)], axis=0)
                    for j in range(3)
                ],
                axis=1,
            )
            part = lax.dot_general(
                lhs, rhs, (((1,), (1,)), ((), ())), preferred_element_type=f32
            )
            total = part if total is None else total + part
        yf[t] = shift_sum(total, WW, OP)[:, :O].astype(bf16).reshape(R, WW, O)
        if t == F + 1:

            @pl.when(has_next)
            def _():
                for d in range(Z):
                    f_next(d).start()

    for d in range(1, Z):
        f_own(d).start()
    rf[z] = yf[pl.ds(0, F), :, mine]

    @pl.when(jnp.logical_not(has_prev))
    def _():
        rp[...] = jnp.zeros_like(rp)

    for d in range(1, Z):
        b_own(d).wait_recv()
    result_b = yb[:, :, mine].astype(f32)
    for d in range(1, Z):
        result_b = result_b + rb[d].astype(f32)
    result_b = result_b.reshape(F * R * W, C)

    for d in range(1, Z):
        f_own(d).wait_recv()

    @pl.when(has_prev)
    def _():
        for d in range(Z):
            f_next(d).wait_recv()

    chunks = []
    for m in range(Z):
        head = rf[m, pl.ds(0, 2)].astype(f32) + rp[m].astype(f32)
        if F > 2:
            head = jnp.concatenate([head, rf[m, pl.ds(2, F - 2)].astype(f32)], axis=0)
        chunks.append(head.reshape(F * R * W, O))
    result_f = jnp.concatenate(chunks, axis=1)

    def drain():
        for d in range(1, Z):
            q_own(d).wait_send()
            x_own(d).wait_send()
            b_own(d).wait_send()
            f_own(d).wait_send()

        @pl.when(has_prev)
        def _():
            for d in range(Z):
                q_prev(d).wait_send()

        @pl.when(has_next)
        def _():
            for d in range(Z):
                f_next(d).wait_send()

        for buf, slot in ((qp, 6 * Z), (xp, 6 * Z + 2)):

            @pl.when(has_high)
            def _():
                to_high(buf, slot).wait_send()

            @pl.when(has_low)
            def _():
                to_low(buf, slot + 1).wait_send()

    return result_f, result_b, drain


def kernel(sizes, latent, cotangent, gain_one, gain_two, kernel_one, kernel_two, out, latent_grad, *scratch):
    S, Q, Z = sizes
    act_one, act_two, grad_two_ref, w_one, w_two, send, recv, w_sem = scratch[:8]
    bufs_one, bufs_two = scratch[8:16], scratch[16:24]
    F, R, W, C = latent.shape
    rows = F * R * W
    s, q, z = lax.axis_index("section"), lax.axis_index("seq"), lax.axis_index("exp")

    load_one = pltpu.make_async_copy(kernel_one, w_one, w_sem.at[0])
    load_two = pltpu.make_async_copy(kernel_two, w_two, w_sem.at[1])
    load_two.start()
    load_one.start()

    barrier = pltpu.get_barrier_semaphore()

    def greet(device):
        pl.semaphore_signal(barrier, inc=1, device_id=device, device_id_type=MESH)

    for d in range(1, Z):
        greet((s, q, lax.rem(z + d, Z)))
    for condition, step in ((s < S - 1, 1), (s > 0, -1)):

        @pl.when(condition)
        def _():
            for d in range(Z):
                greet((s + step, q, lax.rem(z + d, Z)))

    for condition, step in ((q < Q - 1, 1), (q > 0, -1)):

        @pl.when(condition)
        def _():
            greet((s, q + step, z))

    source = latent[...].reshape(rows, C).astype(f32)
    g_one, g_two = gain_one[...], gain_two[...]
    normed_one, inverse_one = normalize(source, g_one)
    act_one[...] = silu(normed_one).astype(bf16).reshape(F, R, W, C)

    sections = (s < S - 1).astype(jnp.int32) + (s > 0).astype(jnp.int32)
    neighbours = (q < Q - 1).astype(jnp.int32) + (q > 0).astype(jnp.int32)
    pl.semaphore_wait(barrier, Z - 1 + Z * sections + neighbours)

    class Done:
        def wait(self):
            pass

    inner, grad_two, drain_one = stage(
        0, sizes, act_one, cotangent, w_one, w_two, bufs_one, send, recv, (load_one, load_two)
    )
    normed_two, inverse_two = normalize(inner, g_two)
    act_two[...] = silu(normed_two).astype(bf16).reshape(F, R, W, C)
    grad_inner = norm_backward(inner, inverse_two, g_two, grad_two * silu_slope(normed_two))
    grad_two_ref[...] = grad_inner.astype(bf16).reshape(F, R, W, C)

    branch, grad_one, drain_two = stage(
        1, sizes, act_two, grad_two_ref, w_two, w_one, bufs_two, send, recv, (Done(), Done())
    )
    source = latent[...].reshape(rows, C).astype(f32)
    out[...] = (source + branch).astype(bf16).reshape(F, R, W, C)
    normed_one, inverse_one = normalize(source, g_one)
    grad = norm_backward(source, inverse_one, g_one, grad_one * silu_slope(normed_one))
    upstream = cotangent[...].reshape(rows, C).astype(f32)
    latent_grad[...] = (upstream + grad).astype(bf16).reshape(F, R, W, C)
    drain_one()
    drain_two()


def local(sizes, latent, cotangent, gain_one, gain_two, kernel_one, kernel_two):
    S, Q, Z = sizes
    F, R, W, C = latent.shape
    O = kernel_one.shape[3]
    WW = W * Z
    block = pltpu.VMEM((F, R, W, C), bf16)
    weight = pltpu.VMEM(kernel_one.shape, bf16)
    bufs = [
        pltpu.VMEM((F, R + 2, WW, C), bf16),
        pltpu.VMEM((Z, F, R, W, O), bf16),
        pltpu.VMEM((F + 2, R + 2, WW, O), bf16),
        pltpu.VMEM((F + 2, R, WW, O), bf16),
        pltpu.VMEM((Z, F, R, W, O), bf16),
        pltpu.VMEM((Z, 2, R, W, O), bf16),
        pltpu.VMEM((F, R, WW, C), bf16),
        pltpu.VMEM((Z, F, R, W, C), bf16),
    ]
    slots = 6 * Z + 4
    vmem = pl.BlockSpec(memory_space=pltpu.VMEM)
    hbm = pl.BlockSpec(memory_space=pl.ANY)
    return pl.pallas_call(
        functools.partial(kernel, sizes),
        out_shape=[jax.ShapeDtypeStruct((F, R, W, C), bf16)] * 2,
        in_specs=[vmem, vmem, vmem, vmem, hbm, hbm],
        out_specs=[vmem, vmem],
        scratch_shapes=[
            block,
            block,
            block,
            weight,
            weight,
            pltpu.SemaphoreType.DMA((2, slots)),
            pltpu.SemaphoreType.DMA((2, slots)),
            pltpu.SemaphoreType.DMA((2,)),
            *bufs,
            *bufs,
        ],
        compiler_params=pltpu.CompilerParams(
            collective_id=0, has_side_effects=True, vmem_limit_bytes=60 * 1024 * 1024
        ),
    )(latent, cotangent, gain_one.reshape(1, C), gain_two.reshape(1, C), kernel_one, kernel_two)


def solution(mesh):
    sizes = (mesh.shape["section"], mesh.shape["seq"], mesh.shape["exp"])
    spread = P("section", "seq", "exp", None)
    split = P(None, None, None, "exp", None)
    return jax.shard_map(
        functools.partial(local, sizes),
        mesh=mesh,
        in_specs=(spread, spread, P(), P(), split, split),
        out_specs=(spread, spread),
        check_vma=False,
    )
```

time: 216 us -> 74.4 us (0.34)
  the two profiles are of different devices: /device:TPU:0 before, /device:TPU:3 now
where the time goes in v1:
time: 74.4 us; the launch traced here: 74.1 us
  Pallas kernels  67.9 us (91%)
  local copies, waits for them, and re-layouts  5.58 us (7%)
    pallas_call x1, Pallas kernels, local(): pl.pallas_call(functools.partial(kernel, sizes), out_shape=[jax.ShapeDtyp...  67.9 us
    unnamed x2, local copies, waits for them, and re-layouts  3.09 us

profile of v1, /device:TPU:3, one launch (start us, length us, event | category | flops | bytes accessed | tf_op | source)
XLA Modules:
  0.0 74.1 jit_solution(3373486871794556240)
XLA Ops:
  0.6 1.2 %reshape.10.gain_one = f32[1,384]{1,0:T(1,128)} reshape(f32[384]{0:T(512)} %param.8) | data formatting | bytes 3072 | tf_op jit(solution)/shard_map/reshape | solution.py:391
  1.9 1.2 %reshape.11.gain_two = f32[1,384]{1,0:T(1,128)} reshape(f32[384]{0:T(512)} %param.9) | data formatting | bytes 3072 | tf_op jit(solution)/shard_map/reshape | solution.py:391
  3.1 67.9 %shard_map.77 = (bf16[2,4,16,384]{3,2,1,0:T(8,128)(2,1)}, bf16[2,4,16,384]{3,2,1,0:T(8,128)(2,1)}) custom-call(bf16[2,4,16,384]{3,2,1,0:T(8,128)(2,1)} %latent.1, bf16[2,4,16,384]{3,2,1,0:T(8,128)(2,1)} %cotangent.1, f32[1,384]{1,0:T(1,128)} %reshape.10.gain_one, f32[1,384]{1,0:T(1,128)} %reshape.11.gain_two, bf16[3,3,3,96,384]{4,3,2,1,0:T(8,128)(2,1)} %kernel_one.1, ...), custom_call_target="tpu_custom_call" | custom-call | tf_op jit(solution)/shard_map/pallas_call | solution.py:371
  71.0 1.5 %copy.10 = bf16[2,4,16,384]{3,2,1,0:T(8,128)(2,1)} copy(bf16[2,4,16,384]{3,2,1,0:T(8,128)(2,1)} %get-tuple-element.4) | data formatting | bytes 196608
  72.6 1.5 %copy.11 = bf16[2,4,16,384]{3,2,1,0:T(8,128)(2,1)} copy(bf16[2,4,16,384]{3,2,1,0:T(8,128)(2,1)} %get-tuple-element.5) | data formatting | bytes 196608

commit v2 on v1

--- a/solution.py
+++ b/solution.py
@@ -83,8 +83,43 @@
             qs.at[peer(d), pl.ds(0, 2)], qp.at[pl.ds(F, 2), body, mine], Z + d, (prv, q, peer(d))
         )
 
-    def x_own(d):
-        return remote(act, xp.at[:, body, mine], 2 * Z + d, (s, q, peer(d)))
+    def block_at(owner):
+        return xp.at[:, body, pl.ds(pl.multiple_of(jnp.clip(owner, 0, Z - 1) * W, W), W)]
+
+    def x_right(k):
+        held = block_at(z - (k - 1))
+        return remote(act if k == 1 else held, held, 2 * Z + k, (s, q, jnp.minimum(z + 1, Z - 1)))
+
+    def x_left(k):
+        held = block_at(z + (k - 1))
+        return remote(act if k == 1 else held, held, 6 * Z + 4 + k, (s, q, jnp.maximum(z - 1, 0)))
+
+    def sends_right(k):
+        return jnp.logical_and(z >= k - 1, z < Z - 1)
+
+    def sends_left(k):
+        return jnp.logical_and(z <= Z - k, z > 0)
+
+    def pass_on(k):
+        @pl.when(sends_right(k))
+        def _():
+            x_right(k).start()
+
+        @pl.when(sends_left(k))
+        def _():
+            x_left(k).start()
+
+    def arrive(k):
+        @pl.when(z >= k)
+        def _():
+            x_right(k).wait_recv()
+
+        @pl.when(z <= Z - 1 - k)
+        def _():
+            x_left(k).wait_recv()
+
+        if k < Z - 1:
+            pass_on(k + 1)
 
     def b_own(d):
         return remote(yb.at[:, :, columns(d)], rb.at[d], 3 * Z + d, (s, q, peer(d)))
@@ -140,8 +175,8 @@
         for d in range(Z):
             q_prev(d).start()
 
-    for d in range(1, Z):
-        x_own(d).start()
+    if Z > 1:
+        pass_on(1)
     qp[pl.ds(0, F), body, mine] = qs[z]
     xp[:, body, mine] = act[...]
 
@@ -158,6 +193,7 @@
             q_prev(d).wait_recv()
 
     exchange_rows(qp, 6 * Z)
+    arrived = 1
     w_ready[1].wait()
 
     def padded(value, axis):
@@ -168,6 +204,9 @@
         return jnp.concatenate([value, jnp.zeros(shape, value.dtype)], axis=axis)
 
     for f in range(F):
+        if arrived < Z:
+            arrive(arrived)
+            arrived += 1
         total = None
         for i in range(3):
             lhs = jnp.concatenate(
@@ -188,8 +227,8 @@
     for d in range(1, Z):
         b_own(d).start()
 
-    for d in range(1, Z):
-        x_own(d).wait_recv()
+    for k in range(arrived, Z):
+        arrive(k)
     exchange_rows(xp, 6 * Z + 2)
     w_ready[0].wait()
     for t in list(range(F, F + 2)) + list(range(F)):
@@ -252,9 +291,18 @@
     result_f = jnp.concatenate(chunks, axis=1)
 
     def drain():
+        for k in range(1, Z):
+
+            @pl.when(sends_right(k))
+            def _():
+                x_right(k).wait_send()
+
+            @pl.when(sends_left(k))
+            def _():
+                x_left(k).wait_send()
+
         for d in range(1, Z):
             q_own(d).wait_send()
-            x_own(d).wait_send()
             b_own(d).wait_send()
             f_own(d).wait_send()
 
@@ -315,7 +363,7 @@
             greet((s, q + step, z))
 
     source = latent[...].reshape(rows, C).astype(f32)
-    g_one, g_two = gain_one[...], gain_two[...]
+    g_one, g_two = gain_one[...].reshape(1, C), gain_two[...].reshape(1, C)
     normed_one, inverse_one = normalize(source, g_one)
     act_one[...] = silu(normed_one).astype(bf16).reshape(F, R, W, C)
 
@@ -365,7 +413,7 @@
         pltpu.VMEM((F, R, WW, C), bf16),
         pltpu.VMEM((Z, F, R, W, C), bf16),
     ]
-    slots = 6 * Z + 4
+    slots = 7 * Z + 4
     vmem = pl.BlockSpec(memory_space=pltpu.VMEM)
     hbm = pl.BlockSpec(memory_space=pl.ANY)
     return pl.pallas_call(
@@ -388,7 +436,7 @@
         compiler_params=pltpu.CompilerParams(
             collective_id=0, has_side_effects=True, vmem_limit_bytes=60 * 1024 * 1024
         ),
-    )(latent, cotangent, gain_one.reshape(1, C), gain_two.reshape(1, C), kernel_one, kernel_two)
+    )(latent, cotangent, gain_one, gain_two, kernel_one, kernel_two)
 
 
 def solution(mesh):

time: 74.4 us -> 73 us (0.981)
  the two profiles are of different devices: /device:TPU:3 before, /device:TPU:0 now
where the time goes in v2:
time: 73 us; the launch traced here: 72.8 us
  Pallas kernels  69.1 us (95%)
  local copies, waits for them, and re-layouts  3.09 us (4%)
    pallas_call x1, Pallas kernels, local(): pl.pallas_call(functools.partial(kernel, sizes), out_shape=[jax.ShapeDtyp...  69.1 us
    unnamed x2, local copies, waits for them, and re-layouts  3.09 us

profile of v2, /device:TPU:0, one launch (start us, length us, event | category | flops | bytes accessed | tf_op | source)
XLA Modules:
  0.0 72.8 jit_solution(6876027047869605908)
XLA Ops:
  0.6 69.1 %shard_map.77 = (bf16[2,4,16,384]{3,2,1,0:T(8,128)(2,1)}, bf16[2,4,16,384]{3,2,1,0:T(8,128)(2,1)}) custom-call(bf16[2,4,16,384]{3,2,1,0:T(8,128)(2,1)} %latent.1, bf16[2,4,16,384]{3,2,1,0:T(8,128)(2,1)} %cotangent.1, f32[384]{0:T(512)} %gain_one.1, f32[384]{0:T(512)} %gain_two.1, bf16[3,3,3,96,384]{4,3,2,1,0:T(8,128)(2,1)} %kernel_one.1, ...), custom_call_target="tpu_custom_call" | custom-call | tf_op jit(solution)/shard_map/pallas_call | solution.py:419
  69.7 1.5 %copy.10 = bf16[2,4,16,384]{3,2,1,0:T(8,128)(2,1)} copy(bf16[2,4,16,384]{3,2,1,0:T(8,128)(2,1)} %get-tuple-element.4) | data formatting | bytes 196608
  71.3 1.5 %copy.11 = bf16[2,4,16,384]{3,2,1,0:T(8,128)(2,1)} copy(bf16[2,4,16,384]{3,2,1,0:T(8,128)(2,1)} %get-tuple-element.5) | data formatting | bytes 196608
